TPU v7x, 32 devices: a whole 2x2x4 slice. The times are simulated.
32 devices in a mesh: prow: 2 (over x), pcol: 16 (over z, y, core).
Axes of the slice: x: 2, y: 2, z: 4, core: 2. Of those that a mesh axis runs over, the one named last changes fastest.
Arguments:
- vectors: float32 [32768, 2048], P('prow', 'pcol'), may hold values from -6 to 6
- reflectors: bfloat16 [4, 256, 32768], P(None, 'pcol', 'prow'), may hold values from -0.03125 to 0.03125
- tau_diag: float32 [4, 256], replicated, may hold values from 0.5 to 1.5
- coupling: float32 [4, 256, 256], replicated, may hold values from -0.375 to 0.375
Outputs:
- result: float32 [32768, 2048], P('prow', 'pcol')
All inputs are finite; a program needn't handle non-finite values.
Results may differ from a plain program's by a relative error of at most 0.0003.
Values may be sent and summed in bfloat16 or wider, within the bound.
A program may use at most 128 MiB of HBM per device.

v0:
```python
import jax
import jax.numpy as jnp
from jax import lax
from jax.sharding import PartitionSpec as P


def on_device(vectors, reflectors, tau_diag, coupling):
    count = reflectors.shape[0]
    gathered = lax.all_gather(reflectors, "pcol", axis=1, tiled=True)
    current = vectors
    for position in range(count - 1, -1, -1):
        rows_panel = gathered[position]
        widened = rows_panel.astype(jnp.float32)
        tri_factor = jnp.diag(tau_diag[position]) + jnp.triu(coupling[position], 1)
        partial_sum = jnp.dot(
            widened, current, precision=lax.Precision.HIGHEST, preferred_element_type=jnp.float32
        )
        totals = lax.psum(partial_sum, "prow")
        updates = jnp.dot(
            tri_factor, totals, precision=lax.Precision.HIGHEST, preferred_element_type=jnp.float32
        )
        current = current - lax.dot_general(
            widened,
            updates,
            (((0,), (0,)), ((), ())),
            precision=lax.Precision.HIGHEST,
            preferred_element_type=jnp.float32,
        )
    return current


def solution(mesh):
    return jax.shard_map(
        on_device,
        mesh=mesh,
        in_specs=(P("prow", "pcol"), P(None, "pcol", "prow"), P(), P()),
        out_specs=P("prow", "pcol"),
        check_vma=False,
    )
```

profile of v0, /device:TPU:0, one launch (start us, length us, event | category | flops | bytes accessed | tf_op | source)
XLA Modules:
  0.0 387.4 jit_solution(3231491931866824591)
XLA Ops:
  6.5 0.7 all-gather.2.cloned.1.call-update
  7.3 0.0 all-reduce.5.cloned.1.call-start
  7.3 9.0 %copy.5 = f32[16384,128]{0,1:T(8,128)} copy(f32[16384,128]{1,0:T(8,128)} %param.4) | data formatting | bytes 16777216 | tf_op args[0]
  16.3 163.4 %all-gather.2.cloned.1.call-done = bf16[4,256,16384]{2,1,0:T(8,128)(2,1)} async-done(((bf16[4,16,16384]{2,1,0:T(8,128)(2,1)}), bf16[4,256,16384]{2,1,0:T(8,128)(2,1)}) %all-gather.2.cloned.1.call-update) | async-done | bytes 33554448 | tf_op jit(solution)/shard_map/all_gather | solution.py:9
  179.7 11.2 %fusion.4 = f32[256,128]{1,0:T(8,128)} fusion(f32[16384,128]{1,0:T(8,128)} %param.4, bf16[4,256,16384]{2,1,0:T(8,128)(2,1)} %all-gather.2.cloned.1.call-done), kind=kOutput, calls=%fused_computation.12 | convolution fusion | flops 6442450944 | bytes 16908288 | tf_op jit(solution)/shard_map/dot_general | solution.py:15
  190.9 0.0 all-reduce.5.cloned.1.call-update
  190.9 0.6 all-reduce.7.cloned.1.call-start
  191.5 21.1 %all-reduce.5.cloned.1.call-done = f32[256,128]{1,0:T(8,128)} async-done(((f32[256,128]{1,0:T(8,128)}), f32[256,128]{1,0:T(8,128)}) %all-reduce.5.cloned.1.call-update) | async-done | bytes 131088 | tf_op jit(solution)/shard_map/psum | solution.py:18
  212.6 1.3 fusion.21
  213.9 9.4 %fusion.3 = f32[16384,128]{0,1:T(8,128)S(1)} fusion(f32[16384,128]{0,1:T(8,128)} %copy.5, f32[256,128]{1,0:T(8,128)S(1)} %fusion.21, bf16[4,256,16384]{2,1,0:T(8,128)(2,1)} %all-gather.2.cloned.1.call-done), kind=kOutput, calls=%fused_computation.7 | convolution fusion | flops 6444548096 | bytes 25296896 | tf_op jit(solution)/shard_map/dot_general | solution.py:22
  223.3 0.0 copy-start
  223.3 3.4 copy-done
  226.7 12.5 %fusion.10 = f32[256,128]{0,1:T(8,128)} fusion(f32[16384,128]{0,1:T(8,128)S(1)} %fusion.3, bf16[4,256,16384]{2,1,0:T(8,128)(2,1)} %all-gather.2.cloned.1.call-done), kind=kOutput, calls=%fused_computation.18 | convolution fusion | flops 6442450944 | bytes 16908288 | tf_op jit(solution)/shard_map/dot_general | solution.py:15
  239.2 0.0 all-reduce.7.cloned.1.call-update
  239.2 0.2 all-reduce.9.cloned.1.call-start
  239.4 21.5 %all-reduce.7.cloned.1.call-done = f32[256,128]{0,1:T(8,128)} async-done(((f32[256,128]{0,1:T(8,128)}), f32[256,128]{0,1:T(8,128)}) %all-reduce.7.cloned.1.call-update) | async-done | bytes 131088 | tf_op jit(solution)/shard_map/psum | solution.py:18
  260.9 1.3 fusion.18
  262.2 9.4 %fusion.2 = f32[16384,128]{0,1:T(8,128)S(1)} fusion(f32[16384,128]{0,1:T(8,128)} %copy-done, f32[256,128]{1,0:T(8,128)S(1)} %fusion.18, bf16[4,256,16384]{2,1,0:T(8,128)(2,1)} %all-gather.2.cloned.1.call-done), kind=kOutput, calls=%fused_computation.5 | convolution fusion | flops 6444548096 | bytes 25296896 | tf_op jit(solution)/shard_map/dot_general | solution.py:22
  271.6 3.4 copy-done.1
  275.0 12.5 %fusion.9 = f32[256,128]{0,1:T(8,128)} fusion(f32[16384,128]{0,1:T(8,128)S(1)} %fusion.2, bf16[4,256,16384]{2,1,0:T(8,128)(2,1)} %all-gather.2.cloned.1.call-done), kind=kOutput, calls=%fused_computation.17 | convolution fusion | flops 6442450944 | bytes 16908288 | tf_op jit(solution)/shard_map/dot_general | solution.py:15
  287.5 0.0 all-reduce.9.cloned.1.call-update
  287.5 0.3 all-reduce.11.cloned.1.call-start
  287.8 21.4 %all-reduce.9.cloned.1.call-done = f32[256,128]{0,1:T(8,128)} async-done(((f32[256,128]{0,1:T(8,128)}), f32[256,128]{0,1:T(8,128)}) %all-reduce.9.cloned.1.call-update) | async-done | bytes 131088 | tf_op jit(solution)/shard_map/psum | solution.py:18
  309.2 1.3 fusion.15
  310.5 9.4 %fusion.1 = f32[16384,128]{0,1:T(8,128)S(1)} fusion(f32[16384,128]{0,1:T(8,128)} %copy-done.1, f32[256,128]{1,0:T(8,128)S(1)} %fusion.15, bf16[4,256,16384]{2,1,0:T(8,128)(2,1)} %all-gather.2.cloned.1.call-done), kind=kOutput, calls=%fused_computation.3 | convolution fusion | flops 6444548096 | bytes 25296896 | tf_op jit(solution)/shard_map/dot_general | solution.py:22
  319.9 3.4 copy-done.2
  323.3 12.5 %fusion.8 = f32[256,128]{0,1:T(8,128)} fusion(f32[16384,128]{0,1:T(8,128)S(1)} %fusion.1, bf16[4,256,16384]{2,1,0:T(8,128)(2,1)} %all-gather.2.cloned.1.call-done), kind=kOutput, calls=%fused_computation.16 | convolution fusion | flops 6442450944 | bytes 16908288 | tf_op jit(solution)/shard_map/dot_general | solution.py:15
  335.7 0.0 all-reduce.11.cloned.1.call-update
  335.8 21.7 %all-reduce.11.cloned.1.call-done = f32[256,128]{0,1:T(8,128)} async-done(((f32[256,128]{0,1:T(8,128)}), f32[256,128]{0,1:T(8,128)}) %all-reduce.11.cloned.1.call-update) | async-done | bytes 131088 | tf_op jit(solution)/shard_map/psum | solution.py:18
  357.5 1.3 fusion.12
  358.8 12.8 %fusion = f32[16384,128]{0,1:T(8,128)} fusion(f32[16384,128]{0,1:T(8,128)} %copy-done.2, f32[256,128]{1,0:T(8,128)S(1)} %fusion.12, bf16[4,256,16384]{2,1,0:T(8,128)(2,1)} %all-gather.2.cloned.1.call-done), kind=kOutput, calls=%fused_computation.1 | convolution fusion | flops 6444548096 | bytes 25296896 | tf_op jit(solution)/shard_map/dot_general | solution.py:22
  371.6 9.0 %copy.6 = f32[16384,128]{1,0:T(8,128)} copy(f32[16384,128]{0,1:T(8,128)} %fusion) | data formatting | bytes 16777216 | tf_op jit(solution)/shard_map/sub | solution.py:22
  (8 shorter events, 0.0 us)
Async XLA Ops:
  6.5 173.1 %all-gather.2.cloned.1.call-start = ((), (), s32[]{:S(2)}) async-start(), calls=%async_computation | async-start | bytes 35651584 | tf_op jit(solution)/shard_map/all_gather | solution.py:9
  7.3 205.4 %all-reduce.5.cloned.1.call-start = ((), (), s32[]{:S(2)}) async-start(), calls=%async_computation.1 | async-start | bytes 262144 | tf_op jit(solution)/shard_map/psum | solution.py:18
  16.3 175.2 %copy-start.3 = (f32[4,256]{1,0:T(4,128)S(1)}, f32[4,256]{1,0:T(4,128)}, u32[]{:S(2)}) copy-start(f32[4,256]{1,0:T(4,128)} %param.6) | copy-start | bytes 12292
  16.3 196.3 %copy-start.4 = (f32[4,256,256]{2,1,0:T(8,128)S(1)}, f32[4,256,256]{2,1,0:T(8,128)}, u32[]{:S(2)}) copy-start(f32[4,256,256]{2,1,0:T(8,128)} %param.7) | copy-start | bytes 3145732
  190.9 70.0 %all-reduce.7.cloned.1.call-start = ((), (), s32[]{:S(2)}) async-start(), calls=%async_computation.2 | async-start | bytes 262144 | tf_op jit(solution)/shard_map/psum | solution.py:18
  223.3 3.4 copy-start
  239.2 70.0 %all-reduce.9.cloned.1.call-start = ((), (), s32[]{:S(2)}) async-start(), calls=%async_computation.3 | async-start | bytes 262144 | tf_op jit(solution)/shard_map/psum | solution.py:18
  271.6 3.4 copy-start.1
  287.5 70.0 %all-reduce.11.cloned.1.call-start = ((), (), s32[]{:S(2)}) async-start(), calls=%async_computation.4 | async-start | bytes 262144 | tf_op jit(solution)/shard_map/psum | solution.py:18
  319.9 3.4 copy-start.2
Sparse Core Ops, SparseCore 0:
  8.9 170.7 all-gather.1
  191.1 21.5 all-reduce.4
  239.3 21.5 all-reduce.6
  287.6 21.5 all-reduce.8
  335.9 21.5 all-reduce.10
where the time goes:
time: 391 us; the launch traced here: 387 us
  waiting for transfers between devices  250 us (64%)
  matrix products  94.8 us (24%)
  local copies, waits for them, and re-layouts  28.2 us (7%)
  between operations  13.5 us (3%)
    all_gather x1, waiting for transfers between devices, on_device(): gathered = lax.all_gather(reflectors, 'pcol', axis=1, tiled=True)  163 us
    psum x4, waiting for transfers between devices, on_device(): totals = lax.psum(partial_sum, 'prow')  85.7 us
    dot_general x4, matrix products, on_device(): jnp.dot(widened, current, precision=lax.Precision.HIGHEST, preferred_elem...  48.7 us
    dot_general x4, matrix products, on_device(): lax.dot_general(widened, updates, (((0,), (0,)), ((), ())), precision=lax...  40.9 us
    unnamed x11, local copies, waits for them, and re-layouts  19.2 us
    sub x1, local copies, waits for them, and re-layouts, on_device(): current - lax.dot_general(widened, updates, (((0,), (0,)), ((), ())), pre...  8.98 us
  transfers between devices with their start and end apart: 5, of which 5 were waited for; matrix products, arithmetic and copies ran while one was open for 2% of the time, Pallas kernels for 0%

commit v1 on v0

--- a/solution.py
+++ b/solution.py
@@ -5,8 +5,12 @@
 
 
 def on_device(vectors, reflectors, tau_diag, coupling):
+
+    def attach_run(array_here):
+        return jnp.concatenate(jax.lax.all_gather(array_here, "pcol"), axis=1)
+
     count = reflectors.shape[0]
-    gathered = lax.all_gather(reflectors, "pcol", axis=1, tiled=True)
+    gathered = attach_run(reflectors)
     current = vectors
     for position in range(count - 1, -1, -1):
         rows_panel = gathered[position]

time: 391 us -> 406 us (1.038)
  local copies, waits for them, and re-layouts: 28.2 us -> 51.6 us
  matrix products: 94.8 us -> 90 us
    slice x0 -> x1, local copies, waits for them, and re-layouts: none -> 20.2 us  [on_device(): rows_panel = gathered[position]]
    dot_general x4, matrix products: 48.7 us -> 44.2 us  [on_device(): jnp.dot(widened, current, precision=lax.Precision.HIGHEST, preferred_elem...]
    unnamed x11 -> x13, local copies, waits for them, and re-layouts: 19.2 us -> 22.4 us
where the time goes in v1:
time: 406 us
  waiting for transfers between devices  250 us (62%)
  matrix products  90 us (22%)
  local copies, waits for them, and re-layouts  51.6 us (13%)
  between operations  13.2 us (3%)
    all_gather x1, waiting for transfers between devices, attach_run(): return jnp.concatenate(jax.lax.all_gather(array_here, 'pcol'), axis=1)  163 us
    psum x4, waiting for transfers between devices, on_device(): totals = lax.psum(partial_sum, 'prow')  86.1 us
    dot_general x4, matrix products, on_device(): jnp.dot(widened, current, precision=lax.Precision.HIGHEST, preferred_elem...  44.2 us
    dot_general x4, matrix products, on_device(): lax.dot_general(widened, updates, (((0,), (0,)), ((), ())), precision=lax...  40.6 us
    unnamed x13, local copies, waits for them, and re-layouts  22.4 us
    slice x1, local copies, waits for them, and re-layouts, on_device(): rows_panel = gathered[position]  20.2 us
    sub x1, local copies, waits for them, and re-layouts, on_device(): current - lax.dot_general(widened, updates, (((0,), (0,)), ((), ())), pre...  8.98 us
  transfers between devices with their start and end apart: 5, of which 5 were waited for; matrix products, arithmetic and copies ran while one was open for 2% of the time, Pallas kernels for 0%

profile of v1, /device:TPU:0, one launch (start us, length us, event | category | flops | bytes accessed | tf_op | source)
XLA Modules:
  0.0 405.8 jit_solution(14707609642674171556)
XLA Ops:
  6.5 0.7 all-gather.3.cloned.1.call-update
  7.3 0.0 all-reduce.5.cloned.1.call-start
  7.3 9.0 %copy.7 = f32[16384,128]{0,1:T(8,128)} copy(f32[16384,128]{1,0:T(8,128)} %param.4) | data formatting | bytes 16777216 | tf_op args[0]
  16.3 163.4 %all-gather.3.cloned.1.call-done = bf16[64,16,16384]{2,1,0:T(8,128)(2,1)} async-done(((bf16[4,16,16384]{2,1,0:T(8,128)(2,1)}), bf16[64,16,16384]{2,1,0:T(8,128)(2,1)}) %all-gather.3.cloned.1.call-update) | async-done | bytes 33554448 | tf_op jit(solution)/shard_map/all_gather | solution.py:10
  179.7 20.2 %fusion.36 = (bf16[1,16,16,16384]{3,2,0,1:T(8,128)(2,1)}, bf16[1,16,16,16384]{3,2,0,1:T(8,128)(2,1)}, bf16[1,16,16,16384]{3,2,0,1:T(8,128)(2,1)}, bf16[1,16,16,16384]{3,2,0,1:T(8,128)(2,1)S(1)}) fusion(bf16[4,16,16,16384]{3,2,0,1:T(8,128)(2,1)} %bitcast.81), kind=kLoop, calls=%fused_computation.45 | loop fusion | bytes 67108864 | tf_op jit(solution)/shard_map/slice | solution.py:16
  200.0 3.2 copy-done.3
  203.2 10.1 %fusion.38 = f32[256,128]{1,0:T(8,128)} fusion(bf16[256,16384]{1,0:T(8,128)(2,1)S(1)} %bitcast.79, f32[16384,128]{1,0:T(8,128)} %param.4), kind=kOutput, calls=%fused_computation.47 | convolution fusion | flops 6442450944 | bytes 16908288 | tf_op jit(solution)/shard_map/dot_general | solution.py:19
  213.3 0.0 all-reduce.5.cloned.1.call-update
  213.3 0.0 all-reduce.7.cloned.1.call-start
  213.4 21.6 %all-reduce.5.cloned.1.call-done = f32[256,128]{1,0:T(8,128)} async-done(((f32[256,128]{1,0:T(8,128)}), f32[256,128]{1,0:T(8,128)}) %all-reduce.5.cloned.1.call-update) | async-done | bytes 131088 | tf_op jit(solution)/shard_map/psum | solution.py:22
  235.0 1.3 fusion.14
  236.3 9.4 %fusion.3 = f32[16384,128]{0,1:T(8,128)S(1)} fusion(f32[16384,128]{0,1:T(8,128)} %copy.7, f32[256,128]{1,0:T(8,128)S(1)} %fusion.14, bf16[256,16384]{1,0:T(8,128)(2,1)} %bitcast.80), kind=kOutput, calls=%fused_computation.7 | convolution fusion | flops 6444548096 | bytes 25296896 | tf_op jit(solution)/shard_map/dot_general | solution.py:26
  245.7 3.4 copy-done
  249.1 11.3 %convolution_bitcast_fusion.6 = f32[256,128]{0,1:T(8,128)} fusion(f32[16384,128]{0,1:T(8,128)S(1)} %fusion.3, bf16[256,16384]{1,0:T(8,128)(2,1)} %bitcast.77), kind=kOutput, calls=%fused_computation.10 | convolution fusion | flops 6442450944 | bytes 16908288 | tf_op jit(solution)/shard_map/dot_general | solution.py:19
  260.4 0.0 all-reduce.7.cloned.1.call-update
  260.5 0.2 all-reduce.9.cloned.1.call-start
  260.7 21.4 %all-reduce.7.cloned.1.call-done = f32[256,128]{0,1:T(8,128)} async-done(((f32[256,128]{0,1:T(8,128)}), f32[256,128]{0,1:T(8,128)}) %all-reduce.7.cloned.1.call-update) | async-done | bytes 131088 | tf_op jit(solution)/shard_map/psum | solution.py:22
  282.1 1.3 fusion.11
  283.5 9.4 %fusion.2 = f32[16384,128]{0,1:T(8,128)S(1)} fusion(f32[16384,128]{0,1:T(8,128)} %copy-done, f32[256,128]{1,0:T(8,128)S(1)} %fusion.11, bf16[256,16384]{1,0:T(8,128)(2,1)} %bitcast.78), kind=kOutput, calls=%fused_computation.5 | convolution fusion | flops 6444548096 | bytes 25296896 | tf_op jit(solution)/shard_map/dot_general | solution.py:26
  292.8 3.4 copy-done.1
  296.2 11.4 %convolution_bitcast_fusion.5 = f32[256,128]{0,1:T(8,128)} fusion(f32[16384,128]{0,1:T(8,128)S(1)} %fusion.2, bf16[256,16384]{1,0:T(8,128)(2,1)} %bitcast.75), kind=kOutput, calls=%fused_computation.9 | convolution fusion | flops 6442450944 | bytes 16908288 | tf_op jit(solution)/shard_map/dot_general | solution.py:19
  307.6 0.0 all-reduce.9.cloned.1.call-update
  307.6 0.3 all-reduce.11.cloned.1.call-start
  307.9 21.4 %all-reduce.9.cloned.1.call-done = f32[256,128]{0,1:T(8,128)} async-done(((f32[256,128]{0,1:T(8,128)}), f32[256,128]{0,1:T(8,128)}) %all-reduce.9.cloned.1.call-update) | async-done | bytes 131088 | tf_op jit(solution)/shard_map/psum | solution.py:22
  329.3 1.3 fusion.8
  330.6 9.4 %fusion.1 = f32[16384,128]{0,1:T(8,128)S(1)} fusion(f32[16384,128]{0,1:T(8,128)} %copy-done.1, f32[256,128]{1,0:T(8,128)S(1)} %fusion.8, bf16[256,16384]{1,0:T(8,128)(2,1)} %bitcast.76), kind=kOutput, calls=%fused_computation.3 | convolution fusion | flops 6444548096 | bytes 25296896 | tf_op jit(solution)/shard_map/dot_general | solution.py:26
  340.0 3.4 copy-done.2
  343.3 11.4 %convolution_bitcast_fusion.4 = f32[256,128]{0,1:T(8,128)} fusion(f32[16384,128]{0,1:T(8,128)S(1)} %fusion.1, bf16[256,16384]{1,0:T(8,128)(2,1)} %bitcast.73), kind=kOutput, calls=%fused_computation.8 | convolution fusion | flops 6442450944 | bytes 16908288 | tf_op jit(solution)/shard_map/dot_general | solution.py:19
  354.7 21.7 %all-reduce.11.cloned.1.call-done = f32[256,128]{0,1:T(8,128)} async-done(((f32[256,128]{0,1:T(8,128)}), f32[256,128]{0,1:T(8,128)}) %all-reduce.11.cloned.1.call-update) | async-done | bytes 131088 | tf_op jit(solution)/shard_map/psum | solution.py:22
  376.4 1.3 fusion.5
  377.7 12.6 %fusion = f32[16384,128]{0,1:T(8,128)} fusion(f32[16384,128]{0,1:T(8,128)} %copy-done.2, f32[256,128]{1,0:T(8,128)S(1)} %fusion.5, bf16[256,16384]{1,0:T(8,128)(2,1)} %bitcast.74), kind=kOutput, calls=%fused_computation.1 | convolution fusion | flops 6444548096 | bytes 25296896 | tf_op jit(solution)/shard_map/dot_general | solution.py:26
  390.3 9.0 %copy.8 = f32[16384,128]{1,0:T(8,128)} copy(f32[16384,128]{0,1:T(8,128)} %fusion) | data formatting | bytes 16777216 | tf_op jit(solution)/shard_map/sub | solution.py:26
  (11 shorter events, 0.0 us)
Async XLA Ops:
  6.5 173.2 %all-gather.3.cloned.1.call-start = ((), (), s32[]{:S(2)}) async-start(), calls=%async_computation.4 | async-start | bytes 35651584 | tf_op jit(solution)/shard_map/all_gather | solution.py:10
  7.3 227.7 %all-reduce.5.cloned.1.call-start = ((), (), s32[]{:S(2)}) async-start(), calls=%async_computation | async-start | bytes 262144 | tf_op jit(solution)/shard_map/psum | solution.py:22
  200.0 3.2 copy-start.3
  203.2 10.2 %copy-start.4 = (f32[4,256]{1,0:T(4,128)S(1)}, f32[4,256]{1,0:T(4,128)}, u32[]{:S(2)}) copy-start(f32[4,256]{1,0:T(4,128)} %param.6) | copy-start | bytes 12292
  203.2 31.8 %copy-start.5 = (f32[4,256,256]{2,1,0:T(8,128)S(1)}, f32[4,256,256]{2,1,0:T(8,128)}, u32[]{:S(2)}) copy-start(f32[4,256,256]{2,1,0:T(8,128)} %param.7) | copy-start | bytes 3145732
  213.3 68.8 %all-reduce.7.cloned.1.call-start = ((), (), s32[]{:S(2)}) async-start(), calls=%async_computation.1 | async-start | bytes 262144 | tf_op jit(solution)/shard_map/psum | solution.py:22
  245.7 3.4 copy-start
  260.5 68.8 %all-reduce.9.cloned.1.call-start = ((), (), s32[]{:S(2)}) async-start(), calls=%async_computation.2 | async-start | bytes 262144 | tf_op jit(solution)/shard_map/psum | solution.py:22
  292.8 3.4 copy-start.1
  307.6 68.8 %all-reduce.11.cloned.1.call-start = ((), (), s32[]{:S(2)}) async-start(), calls=%async_computation.3 | async-start | bytes 262144 | tf_op jit(solution)/shard_map/psum | solution.py:22
  339.9 3.4 copy-start.2
Sparse Core Ops, SparseCore 0:
  8.9 170.7 all-gather.2
  213.4 21.5 all-reduce.4
  260.6 21.5 all-reduce.6
  307.7 21.5 all-reduce.8
  354.8 21.5 all-reduce.10
